TPU v7x, 32 devices: a whole 2x2x4 slice. The times are simulated.
32 devices in a mesh: ta: 16 (over z, y, x), gz: 2 (over core).
Axes of the slice: x: 2, y: 2, z: 4, core: 2. Of those that a mesh axis runs over, the one named last changes fastest.
Arguments:
- time_links: float32 [2, 3, 3, 32, 8, 256], P(None, None, None, 'ta', 'gz'), may hold values from -1 to 1, as said below
- space_links: float32 [3, 2, 3, 3, 32, 8, 256], P(None, None, None, None, 'ta', 'gz'), may hold values from -1 to 1, as said below
Outputs:
- gauge: float32 [2, 3, 3, 32, 8, 256], P(None, None, None, 'ta', 'gz')
- links_fixed: float32 [3, 2, 3, 3, 32, 8, 256], P(None, None, None, None, 'ta', 'gz')
- action_profile: float32 [32, 8], P('ta', 'gz')
- action_mean: float32 [], replicated
Inputs may be any that keep to these rules, and one draw needn't show every extreme that they name: `time_links`: every 3 x 3 complex matrix is unitary up to float32 rounding. `space_links`: every 3 x 3 complex matrix is unitary up to float32 rounding.
All inputs are finite; a program needn't handle non-finite values.
Results may differ from a plain program's by a relative error of at most 0.00024.
Values sent between devices are 32-bit elements; how exact they have to be, the bound alone decides.
No kernel may reach another device: no remote copies, remote signals or barrier semaphores. Data moves between devices by JAX's collectives and lax.ppermute only.
A program may use at most 64 MiB of HBM per device.

v0:
```python
import functools

import jax
import jax.numpy as jnp
from jax import lax
from jax.experimental import pallas as pl
from jax.experimental.pallas import tpu as pltpu
from jax.sharding import PartitionSpec as P


Y = 16


VMEM = pl.BlockSpec(memory_space=pltpu.VMEM)
SMEM = pl.BlockSpec(memory_space=pltpu.SMEM)


def product(a, b):
    out = []
    for i in range(3):
        row = []
        for j in range(3):
            re = im = None
            for k in range(3):
                ar, ai = a[i][k]
                br, bi = b[k][j]
                r = ar * br - ai * bi
                m = ar * bi + ai * br
                re = r if re is None else re + r
                im = m if im is None else im + m
            row.append((re, im))
        out.append(row)
    return out


def product_dagger(a, b):
    out = []
    for i in range(3):
        row = []
        for j in range(3):
            re = im = None
            for k in range(3):
                ar, ai = a[i][k]
                br, bi = b[j][k]
                r = ar * br + ai * bi
                m = ai * br - ar * bi
                re = r if re is None else re + r
                im = m if im is None else im + m
            row.append((re, im))
        out.append(row)
    return out


def mapped(f, *mats):
    return [
        [tuple(f(*(m[i][j][c] for m in mats)) for c in range(2)) for j in range(3)]
        for i in range(3)
    ]


def load(ref, *tail):
    return [[tuple(ref[(c, i, j) + tail] for c in range(2)) for j in range(3)] for i in range(3)]


def store(ref, mat, *tail):
    for i in range(3):
        for j in range(3):
            for c in range(2):
                ref[(c, i, j) + tail] = mat[i][j][c]


def store_low(ref, mat):
    for i in range(3):
        for j in range(3):
            for c in range(2):
                ref[c, i, j] = mat[i][j][c][0:1, :]


def step_x(v):
    return pltpu.roll(v, v.shape[-1] - Y, v.ndim - 1)


def step_y(v):
    n = v.shape[-1]
    lane = lax.broadcasted_iota(jnp.int32, v.shape, v.ndim - 1)
    last = lax.rem(lane, Y) == Y - 1
    ahead = pltpu.roll(v, n - 1, v.ndim - 1)
    back = pltpu.roll(v, Y - 1, v.ndim - 1)
    return jnp.where(last, back, ahead)


def step_z(v, above):
    return jnp.concatenate([v[1:, :], above], axis=0)


def first_kernel(time_ref, space_ref, out_ref, low_ref):
    steps = time_ref.shape[3]
    run = load(time_ref, 0)
    for t in range(1, steps):
        run = product(run, load(time_ref, t))
    store(out_ref, run)
    low_ref[0] = time_ref[..., 0:1, :]
    low_ref[1:3] = space_ref[0:2, ..., 0:1, :]


def group_kernel(radix, digit_ref, *refs):
    slots = refs[:radix]
    total_ref, excl_ref = refs[radix:]
    digit = digit_ref[0]
    for d in range(radix):

        @pl.when(digit == d)
        def _():
            run = None
            for j in range(radix):
                if j == d:
                    if run is None:
                        one = jnp.ones(excl_ref.shape[3:], jnp.float32)
                        zero = jnp.zeros_like(one)
                        excl = [[(one if a == b else zero, zero) for b in range(3)] for a in range(3)]
                        store(excl_ref, excl)
                    else:
                        store(excl_ref, run)
                piece = load(slots[j ^ d])
                run = piece if run is None else product(run, piece)
            store(total_ref, run)


def combine_kernel(has_before, low, bit_ref, mine_ref, other_ref, *refs):
    before_ref = refs[0] if has_before else None
    outs = refs[1:] if has_before else refs
    total_ref, excl_ref = outs[0], outs[1]
    upper = bit_ref[0] == 1

    def finish(total, excl):
        store(total_ref, total)
        store(excl_ref, excl)
        if low:
            store_low(outs[2], total)
            store_low(outs[3], excl)

    @pl.when(upper)
    def _():
        other = load(other_ref)
        excl = product(other, load(before_ref)) if has_before else other
        finish(product(other, load(mine_ref)), excl)

    @pl.when(jnp.logical_not(upper))
    def _():
        if has_before:
            excl = load(before_ref)
        else:
            one = jnp.ones(excl_ref.shape[3:], jnp.float32)
            zero = jnp.zeros_like(one)
            excl = [[(one if a == b else zero, zero) for b in range(3)] for a in range(3)]
        finish(product(load(mine_ref), load(other_ref)), excl)


def plaquette_kernel(space_ref, above_ref, profile_ref, total_ref):
    steps, layers = space_ref.shape[4], space_ref.shape[5]
    sites = space_ref.shape[6]
    eye = (
        lax.broadcasted_iota(jnp.int32, (layers, layers), 0)
        == lax.broadcasted_iota(jnp.int32, (layers, layers), 1)
    )
    whole = jnp.zeros((1, 1), jnp.float32)
    for t in range(steps):
        links = [load(space_ref.at[mu], t) for mu in range(3)]
        above = [load(above_ref.at[mu + 1], t) for mu in range(2)]

        def moved(mu, nu):
            if nu == 0:
                return mapped(step_x, links[mu])
            if nu == 1:
                return mapped(step_y, links[mu])
            return mapped(step_z, links[mu], above[mu])

        density = None
        for mu, nu in ((0, 1), (0, 2), (1, 2)):
            left = product(links[mu], moved(nu, mu))
            right = product(links[nu], moved(mu, nu))
            trace = None
            for i in range(3):
                for j in range(3):
                    term = left[i][j][0] * right[i][j][0] + left[i][j][1] * right[i][j][1]
                    trace = term if trace is None else trace + term
            term = 1.0 - trace / 3.0
            density = term if density is None else density + term
        prof = jnp.sum(density, axis=1, keepdims=True) / (3.0 * sites)
        row = jnp.sum(jnp.where(eye, jnp.broadcast_to(prof, (layers, layers)), 0.0), axis=0, keepdims=True)
        profile_ref[t : t + 1, :] = row
        whole = whole + jnp.sum(row, axis=1, keepdims=True)
    total_ref[...] = jnp.broadcast_to(whole, total_ref.shape)


def final_kernel(
    bit_ref, excl_ref, excl_up_ref, got_ref, got_up_ref, time_ref, time_up_ref, space_ref,
    gauge_ref, fixed_ref, up_ref,
):
    steps = time_ref.shape[3]
    upper = bit_ref[0] == 1

    @pl.when(upper)
    def _():
        store(gauge_ref, product(load(got_ref), load(excl_ref)), 0)
        store(up_ref, product(load(got_up_ref), load(excl_up_ref)))

    @pl.when(jnp.logical_not(upper))
    def _():
        store(gauge_ref, load(excl_ref), 0)
        store(up_ref, load(excl_up_ref))

    for t in range(steps):
        gauge = load(gauge_ref, t)
        above = load(up_ref)
        if t + 1 < steps:
            store(gauge_ref, product(gauge, load(time_ref, t)), t + 1)
            store(up_ref, product(above, load(time_up_ref.at[0], t)))
        for mu in range(3):
            if mu == 0:
                ahead = mapped(step_x, gauge)
            elif mu == 1:
                ahead = mapped(step_y, gauge)
            else:
                ahead = mapped(step_z, gauge, above)
            fixed = product_dagger(product(gauge, load(space_ref.at[mu], t)), ahead)
            store(fixed_ref.at[mu], fixed, t)


def call(kernel, out_shapes, args, smem=0, scratch=(), keep=()):
    return pl.pallas_call(
        kernel,
        out_shape=[
            pltpu.VMEM(s, jnp.float32) if i in keep else jax.ShapeDtypeStruct(s, jnp.float32)
            for i, s in enumerate(out_shapes)
        ],
        in_specs=[SMEM] * smem + [VMEM] * (len(args) - smem),
        out_specs=[VMEM] * len(out_shapes),
        scratch_shapes=list(scratch),
    )(*args)


def near(value):
    return pltpu.with_memory_space_constraint(value, pltpu.VMEM)


def make_on_device(n_ta, n_gz):
    both = ("ta", "gz")
    count = n_ta * n_gz
    bits = n_ta.bit_length() - 1

    def swap(value, axis, n, mask):
        return lax.ppermute(value, axis, [(i, i ^ mask) for i in range(n)])

    def from_upper(value, mask=0):
        pairs = [
            ((i ^ mask) * n_gz + (g + 1) % n_gz, i * n_gz + g) for i in range(n_ta) for g in range(n_gz)
        ]
        return lax.ppermute(value, both, pairs)

    def on_device(time_links, space_links):
        return body(time_links, space_links)

    def body(time_links, space_links):
        steps, layers, sites = time_links.shape[3:]
        mat = (2, 3, 3, layers, sites)
        low = (2, 3, 3, 1, sites)
        me = lax.axis_index("ta")

        def bit(at):
            return ((me >> at) & 1).reshape(1)

        def after(value, *others):
            return lax.optimization_barrier((value,) + others)[0]

        def summed(part, masks):
            parts = [part, swap(part, both, count, masks[0]), swap(part, both, count, masks[1])]
            parts.append(swap(part, both, count, masks[0] ^ masks[1]))
            return (parts[0] + parts[1]) + (parts[2] + parts[3])

        total, lows = call(
            first_kernel,
            [mat, (3,) + time_links.shape[:4] + (1, sites)],
            [time_links, space_links],
            keep=(0, 1),
        )
        slots = [total]
        for mask in (1, 2, 3):
            slots.append(swap(total, "ta", n_ta, mask))
        lows_up = from_upper(lows)
        profile, part = call(
            plaquette_kernel,
            [(steps, layers), (1, 128)],
            [space_links, near(lows_up)],
            keep=(1,),
        )
        args = [(me & 3).reshape(1)] + [near(v) for v in slots]
        total, excl = call(
            functools.partial(group_kernel, 4), [mat, mat], args, 1, keep=range(2)
        )
        left = [1 << at for at in range(count.bit_length() - 1)]
        for at in range(2, bits - 1):
            other = swap(total, "ta", n_ta, 1 << at)
            is_last = at == bits - 2
            if at == 2:
                part = summed(part, left[:2])
                left = left[2:]
                other = after(other, part)
            args = [bit(at)] + [near(v) for v in (total, other, excl)]
            outs = call(
                functools.partial(combine_kernel, True, is_last),
                [mat, mat] + ([low, low] if is_last else []),
                args,
                1,
                keep=range(4),
            )
            total, excl = outs[0], outs[1]
        total_low, excl_low = outs[2], outs[3]
        top = 1 << (bits - 1)
        got = swap(total, "ta", n_ta, top)
        got_up = from_upper(total_low, top)
        excl_up = from_upper(excl_low)
        while len(left) > 1:
            part = summed(part, left[:2])
            left = left[2:]
        got = after(got, part)
        for mask in left:
            more = swap(part, both, count, mask)
            part = part + more
        args = [bit(bits - 1)] + [near(v) for v in (excl, excl_up, got, got_up)]
        args += [time_links, near(lows_up), space_links]
        gauge, fixed = call(
            final_kernel,
            [time_links.shape, space_links.shape],
            args,
            1,
            [pltpu.VMEM(low, jnp.float32)],
        )
        mean = part[0, 0] / (steps * layers * count)
        return gauge, fixed, profile, mean

    return on_device


def solution(mesh):
    return jax.shard_map(
        make_on_device(mesh.shape["ta"], mesh.shape["gz"]),
        mesh=mesh,
        in_specs=(
            P(None, None, None, "ta", "gz", None),
            P(None, None, None, None, "ta", "gz", None),
        ),
        out_specs=(
            P(None, None, None, "ta", "gz", None),
            P(None, None, None, None, "ta", "gz", None),
            P("ta", "gz"),
            P(),
        ),
        check_vma=False,
    )
```

profile of v0, /device:TPU:0, one launch (start us, length us, event | category | flops | bytes accessed | tf_op | source)
XLA Modules:
  0.0 30.5 jit_solution(8359510550538205938)
XLA Ops:
  0.6 1.2 %shard_map.57 = (f32[2,3,3,4,256]{4,3,2,1,0:T(4,128)S(1)}, f32[3,2,3,3,2,1,256]{6,5,4,3,2,1,0:T(1,128)S(1)}) custom-call(f32[2,3,3,2,4,256]{5,4,3,2,1,0:T(4,128)} %time_ref.3, f32[3,2,3,3,2,4,256]{6,5,4,3,2,1,0:T(4,128)} %space_ref.5), custom_call_target="tpu_custom_call" | custom-call | tf_op jit(solution)/shard_map/pallas_call | solution.py:231
  1.8 0.6 %collective-permute-start.4 = (f32[3,2,3,3,2,1,256]{6,5,4,3,2,1,0:T(1,128)S(1)}, f32[3,2,3,3,2,1,256]{6,5,4,3,2,1,0:T(1,128)S(1)}, u32[]{:S(2)}, u32[]{:S(2)}) collective-permute-start(f32[3,2,3,3,2,1,256]{6,5,4,3,2,1,0:T(1,128)S(1)} %get-tuple-element.20), channel_id=1, source_target_pairs={{1,0},{0,1},{3,2},{2,3},{5,4},{4,5},{7,6},{6,7},{9,8},{8,9},{11,10... | collective-permute-start | bytes 331784 | tf_op jit(solution)/shard_map/ppermute | solution.py:259
  2.4 3.5 %collective-permute-start.2 = (f32[2,3,3,4,256]{4,3,2,1,0:T(4,128)S(1)}, f32[2,3,3,4,256]{4,3,2,1,0:T(4,128)S(1)}, u32[]{:S(2)}, u32[]{:S(2)}) collective-permute-start(f32[2,3,3,4,256]{4,3,2,1,0:T(4,128)S(1)} %get-tuple-element.18.refs_0_), channel_id=1, source_target_pairs={{0,6},{2,4},{4,2},{6,0},{8,14},{10,12},{12,10},{14,8},{16,22},{18,... | collective-permute-start | bytes 221192 | tf_op jit(solution)/shard_map/ppermute | solution.py:253
  5.9 0.5 %collective-permute-start.1 = (f32[2,3,3,4,256]{4,3,2,1,0:T(4,128)S(1)}, f32[2,3,3,4,256]{4,3,2,1,0:T(4,128)S(1)}, u32[]{:S(2)}, u32[]{:S(2)}) collective-permute-start(f32[2,3,3,4,256]{4,3,2,1,0:T(4,128)S(1)} %get-tuple-element.18.refs_0_), channel_id=1, source_target_pairs={{0,4},{2,6},{4,0},{6,2},{8,12},{10,14},{12,8},{14,10},{16,20},{18,... | collective-permute-start | bytes 221192 | tf_op jit(solution)/shard_map/ppermute | solution.py:253
  6.4 0.1 collective-permute-start
  6.5 0.0 collective-permute-done.4.above_ref.time_up_ref
  6.5 2.4 %shard_map.59 = (f32[2,4]{1,0:T(2,128)}, f32[1,128]{1,0:T(1,128)S(1)}) custom-call(f32[3,2,3,3,2,4,256]{6,5,4,3,2,1,0:T(4,128)} %space_ref.5, f32[3,2,3,3,2,1,256]{6,5,4,3,2,1,0:T(1,128)S(1)} %collective-permute-done.4.above_ref.time_up_ref), custom_call_target="tpu_custom_call" | custom-call | tf_op jit(solution)/shard_map/pallas_call | solution.py:231
  8.9 1.1 %collective-permute-start.7 = (f32[1,128]{1,0:T(1,128)S(1)}, f32[1,128]{1,0:T(1,128)S(1)}, u32[]{:S(2)}, u32[]{:S(2)}) collective-permute-start(f32[1,128]{1,0:T(1,128)S(1)} %get-tuple-element.21), channel_id=1, source_target_pairs={{0,3},{1,2},{2,1},{3,0},{4,7},{5,6},{6,5},{7,4},{8,11},{9,10},{10,... | collective-permute-start | bytes 1544 | tf_op jit(solution)/shard_map/ppermute | solution.py:253
  10.0 0.8 %collective-permute-start.6 = (f32[1,128]{1,0:T(1,128)S(1)}, f32[1,128]{1,0:T(1,128)S(1)}, u32[]{:S(2)}, u32[]{:S(2)}) collective-permute-start(f32[1,128]{1,0:T(1,128)S(1)} %get-tuple-element.21), channel_id=1, source_target_pairs={{0,2},{1,3},{2,0},{3,1},{4,6},{5,7},{6,4},{7,5},{8,10},{9,11},{10,... | collective-permute-start | bytes 1544 | tf_op jit(solution)/shard_map/ppermute | solution.py:253
  10.8 0.0 collective-permute-done.2.refs_3_
  10.8 0.1 collective-permute-start.5
  10.9 0.0 collective-permute-done.1.refs_2_
  10.9 0.0 collective-permute-done.refs_1_
  10.9 0.1 shard_map.58
  11.0 1.9 %collective-permute-start.3 = (f32[2,3,3,4,256]{4,3,2,1,0:T(4,128)S(1)}, f32[2,3,3,4,256]{4,3,2,1,0:T(4,128)S(1)}, u32[]{:S(2)}, u32[]{:S(2)}) collective-permute-start(f32[2,3,3,4,256]{4,3,2,1,0:T(4,128)S(1)} %get-tuple-element.19.mine_ref), channel_id=1, source_target_pairs={{0,8},{2,10},{4,12},{6,14},{8,0},{10,2},{12,4},{14,6},{16,24},{18,... | collective-permute-start | bytes 221192 | tf_op jit(solution)/shard_map/ppermute | solution.py:253
  12.9 0.0 collective-permute-done.7
  12.9 0.6 %collective-permute-done.6 = f32[1,128]{1,0:T(1,128)S(1)} collective-permute-done((f32[1,128]{1,0:T(1,128)S(1)}, f32[1,128]{1,0:T(1,128)S(1)}, u32[]{:S(2)}, u32[]{:S(2)}) %collective-permute-start.6) | collective-permute-done | bytes 544 | tf_op jit(solution)/shard_map/ppermute | solution.py:253
  13.6 0.0 collective-permute-done.5
  13.6 2.6 %collective-permute-start.12 = (f32[1,128]{1,0:T(1,128)S(1)}, f32[1,128]{1,0:T(1,128)S(1)}, u32[]{:S(2)}, u32[]{:S(2)}) collective-permute-start(f32[1,128]{1,0:T(1,128)S(1)} %add_add_fusion.1), channel_id=1, source_target_pairs={{0,12},{1,13},{2,14},{3,15},{4,8},{5,9},{6,10},{7,11},{8,4},{9,5},... | collective-permute-start | bytes 1544 | tf_op jit(solution)/shard_map/ppermute | solution.py:253
  16.2 0.4 %collective-permute-start.11 = (f32[1,128]{1,0:T(1,128)S(1)}, f32[1,128]{1,0:T(1,128)S(1)}, u32[]{:S(2)}, u32[]{:S(2)}) collective-permute-start(f32[1,128]{1,0:T(1,128)S(1)} %add_add_fusion.1), channel_id=1, source_target_pairs={{0,8},{1,9},{2,10},{3,11},{4,12},{5,13},{6,14},{7,15},{8,0},{9,1},... | collective-permute-start | bytes 1544 | tf_op jit(solution)/shard_map/ppermute | solution.py:253
  16.6 0.5 %collective-permute-start.10 = (f32[1,128]{1,0:T(1,128)S(1)}, f32[1,128]{1,0:T(1,128)S(1)}, u32[]{:S(2)}, u32[]{:S(2)}) collective-permute-start(f32[1,128]{1,0:T(1,128)S(1)} %add_add_fusion.1), channel_id=1, source_target_pairs={{0,4},{1,5},{2,6},{3,7},{4,0},{5,1},{6,2},{7,3},{8,12},{9,13},{10,... | collective-permute-start | bytes 1544 | tf_op jit(solution)/shard_map/ppermute | solution.py:253
  17.1 0.0 collective-permute-done.3.other_ref
  17.2 0.1 collective-permute-start.8
  17.3 2.7 %collective-permute-start.13 = (f32[2,3,3,1,256]{4,3,2,1,0:T(1,128)S(1)}, f32[2,3,3,1,256]{4,3,2,1,0:T(1,128)S(1)}, u32[]{:S(2)}, u32[]{:S(2)}) collective-permute-start(f32[2,3,3,1,256]{4,3,2,1,0:T(1,128)S(1)} %get-tuple-element.28), channel_id=1, source_target_pairs={{17,0},{16,1},{19,2},{18,3},{21,4},{20,5},{23,6},{22,7},{25,8},{24... | collective-permute-start | bytes 55304 | tf_op jit(solution)/shard_map/ppermute | solution.py:259
  20.0 0.7 %collective-permute-start.9 = (f32[2,3,3,4,256]{4,3,2,1,0:T(4,128)S(1)}, f32[2,3,3,4,256]{4,3,2,1,0:T(4,128)S(1)}, u32[]{:S(2)}, u32[]{:S(2)}) collective-permute-start(f32[2,3,3,4,256]{4,3,2,1,0:T(4,128)S(1)} %get-tuple-element.26), channel_id=1, source_target_pairs={{0,16},{2,18},{4,20},{6,22},{8,24},{10,26},{12,28},{14,30},{16,0},... | collective-permute-start | bytes 221192 | tf_op jit(solution)/shard_map/ppermute | solution.py:253
  20.7 0.0 collective-permute-done.11
  20.7 0.0 collective-permute-done.10
  20.7 2.3 %collective-permute-start.14 = (f32[1,128]{1,0:T(1,128)S(1)}, f32[1,128]{1,0:T(1,128)S(1)}, u32[]{:S(2)}, u32[]{:S(2)}) collective-permute-start(f32[1,128]{1,0:T(1,128)S(1)} %add_add_fusion), channel_id=1, source_target_pairs={{0,16},{1,17},{2,18},{3,19},{4,20},{5,21},{6,22},{7,23},{8,24},{9,... | collective-permute-start | bytes 1544 | tf_op jit(solution)/shard_map/ppermute | solution.py:253
  23.0 3.9 %collective-permute-done.14 = f32[1,128]{1,0:T(1,128)S(1)} collective-permute-done((f32[1,128]{1,0:T(1,128)S(1)}, f32[1,128]{1,0:T(1,128)S(1)}, u32[]{:S(2)}, u32[]{:S(2)}) %collective-permute-start.14) | collective-permute-done | bytes 544 | tf_op jit(solution)/shard_map/ppermute | solution.py:253
  27.0 0.0 collective-permute-done.8.excl_up_ref
  27.0 0.0 collective-permute-done.13.got_up_ref
  27.0 2.4 %shard_map.61 = (f32[2,3,3,2,4,256]{5,4,3,2,1,0:T(4,128)}, f32[3,2,3,3,2,4,256]{6,5,4,3,2,1,0:T(4,128)}) custom-call(s32[1]{0:T(128)} %bitcast.bit_ref, f32[2,3,3,4,256]{4,3,2,1,0:T(4,128)S(1)} %get-tuple-element.24.excl_ref, f32[2,3,3,1,256]{4,3,2,1,0:T(1,128)S(1)} %collective-permute-done.8.excl_up_ref, ...), custom_call_target="tpu_custom_call" | custom-call | tf_op jit(solution)/shard_map/pallas_call | solution.py:231
  (6 shorter events, 0.1 us)
Async XLA Ops:
  1.8 4.7 %collective-permute-start.4 = (f32[3,2,3,3,2,1,256]{6,5,4,3,2,1,0:T(1,128)S(1)}, f32[3,2,3,3,2,1,256]{6,5,4,3,2,1,0:T(1,128)S(1)}, u32[]{:S(2)}, u32[]{:S(2)}) collective-permute-start(f32[3,2,3,3,2,1,256]{6,5,4,3,2,1,0:T(1,128)S(1)} %get-tuple-element.20), channel_id=1, source_target_pairs={{1,0},{0,1},{3,2},{2,3},{5,4},{4,5},{7,6},{6,7},{9,8},{8,9},{11,10... | collective-permute-start | bytes 331784 | tf_op jit(solution)/shard_map/ppermute | solution.py:259
  2.4 8.5 %collective-permute-start.2 = (f32[2,3,3,4,256]{4,3,2,1,0:T(4,128)S(1)}, f32[2,3,3,4,256]{4,3,2,1,0:T(4,128)S(1)}, u32[]{:S(2)}, u32[]{:S(2)}) collective-permute-start(f32[2,3,3,4,256]{4,3,2,1,0:T(4,128)S(1)} %get-tuple-element.18.refs_0_), channel_id=1, source_target_pairs={{0,6},{2,4},{4,2},{6,0},{8,14},{10,12},{12,10},{14,8},{16,22},{18,... | collective-permute-start | bytes 221192 | tf_op jit(solution)/shard_map/ppermute | solution.py:253
  5.9 5.1 %collective-permute-start.1 = (f32[2,3,3,4,256]{4,3,2,1,0:T(4,128)S(1)}, f32[2,3,3,4,256]{4,3,2,1,0:T(4,128)S(1)}, u32[]{:S(2)}, u32[]{:S(2)}) collective-permute-start(f32[2,3,3,4,256]{4,3,2,1,0:T(4,128)S(1)} %get-tuple-element.18.refs_0_), channel_id=1, source_target_pairs={{0,4},{2,6},{4,0},{6,2},{8,12},{10,14},{12,8},{14,10},{16,20},{18,... | collective-permute-start | bytes 221192 | tf_op jit(solution)/shard_map/ppermute | solution.py:253
  6.4 4.6 %collective-permute-start = (f32[2,3,3,4,256]{4,3,2,1,0:T(4,128)S(1)}, f32[2,3,3,4,256]{4,3,2,1,0:T(4,128)S(1)}, u32[]{:S(2)}, u32[]{:S(2)}) collective-permute-start(f32[2,3,3,4,256]{4,3,2,1,0:T(4,128)S(1)} %get-tuple-element.18.refs_0_), channel_id=1, source_target_pairs={{0,2},{2,0},{4,6},{6,4},{8,10},{10,8},{12,14},{14,12},{16,18},{18,... | collective-permute-start | bytes 221192 | tf_op jit(solution)/shard_map/ppermute | solution.py:253
  8.9 4.0 %collective-permute-start.7 = (f32[1,128]{1,0:T(1,128)S(1)}, f32[1,128]{1,0:T(1,128)S(1)}, u32[]{:S(2)}, u32[]{:S(2)}) collective-permute-start(f32[1,128]{1,0:T(1,128)S(1)} %get-tuple-element.21), channel_id=1, source_target_pairs={{0,3},{1,2},{2,1},{3,0},{4,7},{5,6},{6,5},{7,4},{8,11},{9,10},{10,... | collective-permute-start | bytes 1544 | tf_op jit(solution)/shard_map/ppermute | solution.py:253
  10.0 3.6 %collective-permute-start.6 = (f32[1,128]{1,0:T(1,128)S(1)}, f32[1,128]{1,0:T(1,128)S(1)}, u32[]{:S(2)}, u32[]{:S(2)}) collective-permute-start(f32[1,128]{1,0:T(1,128)S(1)} %get-tuple-element.21), channel_id=1, source_target_pairs={{0,2},{1,3},{2,0},{3,1},{4,6},{5,7},{6,4},{7,5},{8,10},{9,11},{10,... | collective-permute-start | bytes 1544 | tf_op jit(solution)/shard_map/ppermute | solution.py:253
  10.8 2.8 %collective-permute-start.5 = (f32[1,128]{1,0:T(1,128)S(1)}, f32[1,128]{1,0:T(1,128)S(1)}, u32[]{:S(2)}, u32[]{:S(2)}) collective-permute-start(f32[1,128]{1,0:T(1,128)S(1)} %get-tuple-element.21), channel_id=1, source_target_pairs={{0,1},{1,0},{2,3},{3,2},{4,5},{5,4},{6,7},{7,6},{8,9},{9,8},{10,11... | collective-permute-start | bytes 1544 | tf_op jit(solution)/shard_map/ppermute | solution.py:253
  11.0 6.1 %collective-permute-start.3 = (f32[2,3,3,4,256]{4,3,2,1,0:T(4,128)S(1)}, f32[2,3,3,4,256]{4,3,2,1,0:T(4,128)S(1)}, u32[]{:S(2)}, u32[]{:S(2)}) collective-permute-start(f32[2,3,3,4,256]{4,3,2,1,0:T(4,128)S(1)} %get-tuple-element.19.mine_ref), channel_id=1, source_target_pairs={{0,8},{2,10},{4,12},{6,14},{8,0},{10,2},{12,4},{14,6},{16,24},{18,... | collective-permute-start | bytes 221192 | tf_op jit(solution)/shard_map/ppermute | solution.py:253
  13.6 6.4 %collective-permute-start.12 = (f32[1,128]{1,0:T(1,128)S(1)}, f32[1,128]{1,0:T(1,128)S(1)}, u32[]{:S(2)}, u32[]{:S(2)}) collective-permute-start(f32[1,128]{1,0:T(1,128)S(1)} %add_add_fusion.1), channel_id=1, source_target_pairs={{0,12},{1,13},{2,14},{3,15},{4,8},{5,9},{6,10},{7,11},{8,4},{9,5},... | collective-permute-start | bytes 1544 | tf_op jit(solution)/shard_map/ppermute | solution.py:253
  16.2 4.5 %collective-permute-start.11 = (f32[1,128]{1,0:T(1,128)S(1)}, f32[1,128]{1,0:T(1,128)S(1)}, u32[]{:S(2)}, u32[]{:S(2)}) collective-permute-start(f32[1,128]{1,0:T(1,128)S(1)} %add_add_fusion.1), channel_id=1, source_target_pairs={{0,8},{1,9},{2,10},{3,11},{4,12},{5,13},{6,14},{7,15},{8,0},{9,1},... | collective-permute-start | bytes 1544 | tf_op jit(solution)/shard_map/ppermute | solution.py:253
  16.6 4.1 %collective-permute-start.10 = (f32[1,128]{1,0:T(1,128)S(1)}, f32[1,128]{1,0:T(1,128)S(1)}, u32[]{:S(2)}, u32[]{:S(2)}) collective-permute-start(f32[1,128]{1,0:T(1,128)S(1)} %add_add_fusion.1), channel_id=1, source_target_pairs={{0,4},{1,5},{2,6},{3,7},{4,0},{5,1},{6,2},{7,3},{8,12},{9,13},{10,... | collective-permute-start | bytes 1544 | tf_op jit(solution)/shard_map/ppermute | solution.py:253
  17.2 9.8 %collective-permute-start.8 = (f32[2,3,3,1,256]{4,3,2,1,0:T(1,128)S(1)}, f32[2,3,3,1,256]{4,3,2,1,0:T(1,128)S(1)}, u32[]{:S(2)}, u32[]{:S(2)}) collective-permute-start(f32[2,3,3,1,256]{4,3,2,1,0:T(1,128)S(1)} %get-tuple-element.25), channel_id=1, source_target_pairs={{1,0},{0,1},{3,2},{2,3},{5,4},{4,5},{7,6},{6,7},{9,8},{8,9},{11,10... | collective-permute-start | bytes 55304 | tf_op jit(solution)/shard_map/ppermute | solution.py:259
  17.3 9.7 %collective-permute-start.13 = (f32[2,3,3,1,256]{4,3,2,1,0:T(1,128)S(1)}, f32[2,3,3,1,256]{4,3,2,1,0:T(1,128)S(1)}, u32[]{:S(2)}, u32[]{:S(2)}) collective-permute-start(f32[2,3,3,1,256]{4,3,2,1,0:T(1,128)S(1)} %get-tuple-element.28), channel_id=1, source_target_pairs={{17,0},{16,1},{19,2},{18,3},{21,4},{20,5},{23,6},{22,7},{25,8},{24... | collective-permute-start | bytes 55304 | tf_op jit(solution)/shard_map/ppermute | solution.py:259
  20.0 7.0 %collective-permute-start.9 = (f32[2,3,3,4,256]{4,3,2,1,0:T(4,128)S(1)}, f32[2,3,3,4,256]{4,3,2,1,0:T(4,128)S(1)}, u32[]{:S(2)}, u32[]{:S(2)}) collective-permute-start(f32[2,3,3,4,256]{4,3,2,1,0:T(4,128)S(1)} %get-tuple-element.26), channel_id=1, source_target_pairs={{0,16},{2,18},{4,20},{6,22},{8,24},{10,26},{12,28},{14,30},{16,0},... | collective-permute-start | bytes 221192 | tf_op jit(solution)/shard_map/ppermute | solution.py:253
  20.7 6.2 %collective-permute-start.14 = (f32[1,128]{1,0:T(1,128)S(1)}, f32[1,128]{1,0:T(1,128)S(1)}, u32[]{:S(2)}, u32[]{:S(2)}) collective-permute-start(f32[1,128]{1,0:T(1,128)S(1)} %add_add_fusion), channel_id=1, source_target_pairs={{0,16},{1,17},{2,18},{3,19},{4,20},{5,21},{6,22},{7,23},{8,24},{9,... | collective-permute-start | bytes 1544 | tf_op jit(solution)/shard_map/ppermute | solution.py:253
where the time goes:
time: 30.7 us; the launch traced here: 30.5 us
  starting transfers between devices  17.9 us (58%)
  Pallas kernels  6.09 us (20%)
  waiting for transfers between devices  4.6 us (15%)
  between operations  1.87 us (6%)
    ppermute x12, starting transfers between devices, swap(): return lax.ppermute(value, axis, [(i, i ^ mask) for i in range(n)])  14.6 us
    pallas_call x5, Pallas kernels, call(): pl.pallas_call(kernel, out_shape=[pltpu.VMEM(s, jnp.float32) if i in keep...  6.09 us
    ppermute x12, waiting for transfers between devices, swap(): return lax.ppermute(value, axis, [(i, i ^ mask) for i in range(n)])  4.59 us
    ppermute x3, starting transfers between devices, from_upper(): return lax.ppermute(value, both, pairs)  3.32 us
  transfers between devices with their start and end apart: 15, of which 2 were waited for; matrix products, arithmetic and copies ran while one was open for 0% of the time, Pallas kernels for 8%

commit v1 on v0

--- a/solution.py
+++ b/solution.py
@@ -76,6 +76,39 @@
                 ref[c, i, j] = mat[i][j][c][0:1, :]
 
 
+def times(a, b):
+    return a[0] * b[0] - a[1] * b[1], a[0] * b[1] + a[1] * b[0]
+
+
+def cross(mat):
+    out = []
+    for j in range(3):
+        k, m = (j + 1) % 3, (j + 2) % 3
+        p = times(mat[0][k], mat[1][m])
+        q = times(mat[0][m], mat[1][k])
+        out.append((p[0] - q[0], p[1] - q[1]))
+    return out
+
+
+def pack(ref, mat):
+    for i in range(2):
+        for j in range(3):
+            for c in range(2):
+                ref[i * 6 + j * 2 + c] = mat[i][j][c]
+    terms = [times(mat[2][j], v) for j, v in enumerate(cross(mat))]
+    for c in range(2):
+        ref[12 + c] = terms[0][c] + terms[1][c] + terms[2][c]
+
+
+def unpack(ref):
+    rows = [
+        [tuple(ref[i * 6 + j * 2 + c] for c in range(2)) for j in range(3)] for i in range(2)
+    ]
+    det = (ref[12], ref[13])
+    rows.append([times(det, (v[0], -v[1])) for v in cross(rows)])
+    return rows
+
+
 def step_x(v):
     return pltpu.roll(v, v.shape[-1] - Y, v.ndim - 1)
 
@@ -98,7 +131,7 @@
     run = load(time_ref, 0)
     for t in range(1, steps):
         run = product(run, load(time_ref, t))
-    store(out_ref, run)
+    pack(out_ref, run)
     low_ref[0] = time_ref[..., 0:1, :]
     low_ref[1:3] = space_ref[0:2, ..., 0:1, :]
 
@@ -121,9 +154,9 @@
                         store(excl_ref, excl)
                     else:
                         store(excl_ref, run)
-                piece = load(slots[j ^ d])
+                piece = unpack(slots[j ^ d])
                 run = piece if run is None else product(run, piece)
-            store(total_ref, run)
+            pack(total_ref, run)
 
 
 def combine_kernel(has_before, low, bit_ref, mine_ref, other_ref, *refs):
@@ -133,7 +166,7 @@
     upper = bit_ref[0] == 1
 
     def finish(total, excl):
-        store(total_ref, total)
+        pack(total_ref, total)
         store(excl_ref, excl)
         if low:
             store_low(outs[2], total)
@@ -141,9 +174,9 @@
 
     @pl.when(upper)
     def _():
-        other = load(other_ref)
+        other = unpack(other_ref)
         excl = product(other, load(before_ref)) if has_before else other
-        finish(product(other, load(mine_ref)), excl)
+        finish(product(other, unpack(mine_ref)), excl)
 
     @pl.when(jnp.logical_not(upper))
     def _():
@@ -153,7 +186,7 @@
             one = jnp.ones(excl_ref.shape[3:], jnp.float32)
             zero = jnp.zeros_like(one)
             excl = [[(one if a == b else zero, zero) for b in range(3)] for a in range(3)]
-        finish(product(load(mine_ref), load(other_ref)), excl)
+        finish(product(unpack(mine_ref), unpack(other_ref)), excl)
 
 
 def plaquette_kernel(space_ref, above_ref, profile_ref, total_ref):
@@ -202,7 +235,7 @@
 
     @pl.when(upper)
     def _():
-        store(gauge_ref, product(load(got_ref), load(excl_ref)), 0)
+        store(gauge_ref, product(unpack(got_ref), load(excl_ref)), 0)
         store(up_ref, product(load(got_up_ref), load(excl_up_ref)))
 
     @pl.when(jnp.logical_not(upper))
@@ -264,23 +297,22 @@
     def body(time_links, space_links):
         steps, layers, sites = time_links.shape[3:]
         mat = (2, 3, 3, layers, sites)
+        packed = (14, layers, sites)
         low = (2, 3, 3, 1, sites)
         me = lax.axis_index("ta")
 
         def bit(at):
             return ((me >> at) & 1).reshape(1)
-
-        def after(value, *others):
-            return lax.optimization_barrier((value,) + others)[0]
 
         def summed(part, masks):
             parts = [part, swap(part, both, count, masks[0]), swap(part, both, count, masks[1])]
             parts.append(swap(part, both, count, masks[0] ^ masks[1]))
             return (parts[0] + parts[1]) + (parts[2] + parts[3])
 
+        space_near = near(space_links)
         total, lows = call(
             first_kernel,
-            [mat, (3,) + time_links.shape[:4] + (1, sites)],
+            [packed, (3,) + time_links.shape[:4] + (1, sites)],
             [time_links, space_links],
             keep=(0, 1),
         )
@@ -291,25 +323,23 @@
         profile, part = call(
             plaquette_kernel,
             [(steps, layers), (1, 128)],
-            [space_links, near(lows_up)],
+            [space_near, near(lows_up)],
             keep=(1,),
         )
         args = [(me & 3).reshape(1)] + [near(v) for v in slots]
         total, excl = call(
-            functools.partial(group_kernel, 4), [mat, mat], args, 1, keep=range(2)
+            functools.partial(group_kernel, 4), [packed, mat], args, 1, keep=range(2)
         )
         left = [1 << at for at in range(count.bit_length() - 1)]
+        part = summed(part, left[:2])
+        left = left[2:]
         for at in range(2, bits - 1):
+            is_last = at == bits - 2
             other = swap(total, "ta", n_ta, 1 << at)
-            is_last = at == bits - 2
-            if at == 2:
-                part = summed(part, left[:2])
-                left = left[2:]
-                other = after(other, part)
             args = [bit(at)] + [near(v) for v in (total, other, excl)]
             outs = call(
                 functools.partial(combine_kernel, True, is_last),
-                [mat, mat] + ([low, low] if is_last else []),
+                [packed, mat] + ([low, low] if is_last else []),
                 args,
                 1,
                 keep=range(4),
@@ -323,12 +353,11 @@
         while len(left) > 1:
             part = summed(part, left[:2])
             left = left[2:]
-        got = after(got, part)
         for mask in left:
             more = swap(part, both, count, mask)
             part = part + more
         args = [bit(bits - 1)] + [near(v) for v in (excl, excl_up, got, got_up)]
-        args += [time_links, near(lows_up), space_links]
+        args += [near(time_links), near(lows_up), space_near]
         gauge, fixed = call(
             final_kernel,
             [time_links.shape, space_links.shape],

time: 30.7 us -> 27.1 us (0.88)
  Pallas kernels: 6.09 us -> 4.12 us
  waiting for transfers between devices: 4.6 us -> 3.39 us
  starting transfers between devices: 17.9 us -> 17.5 us
    ppermute x3, starting transfers between devices: 3.32 us -> 0.72 us  [from_upper(): return lax.ppermute(value, both, pairs)]
    ppermute x12, starting transfers between devices: 14.6 us -> 16.7 us  [swap(): return lax.ppermute(value, axis, [(i, i ^ mask) for i in range(n)])]
    pallas_call x5, Pallas kernels: 6.09 us -> 4.12 us  [call(): pl.pallas_call(kernel, out_shape=[pltpu.VMEM(s, jnp.float32) if i in keep...]
    ppermute x12, waiting for transfers between devices: 4.59 us -> 3.38 us  [swap(): return lax.ppermute(value, axis, [(i, i ^ mask) for i in range(n)])]
  transfers between devices with their start and end apart: 15 -> 15, of which waited for: 2 -> 2; matrix products, arithmetic and copies ran while one was open for 0% -> 0% of each run, Pallas kernels for 8% -> 6%
where the time goes in v1:
time: 27.1 us; the launch traced here: 26.9 us
  starting transfers between devices  17.5 us (65%)
  Pallas kernels  4.12 us (15%)
  waiting for transfers between devices  3.39 us (13%)
  between operations  1.91 us (7%)
    ppermute x12, starting transfers between devices, swap(): return lax.ppermute(value, axis, [(i, i ^ mask) for i in range(n)])  16.7 us
    pallas_call x5, Pallas kernels, call(): pl.pallas_call(kernel, out_shape=[pltpu.VMEM(s, jnp.float32) if i in keep...  4.12 us
    ppermute x12, waiting for transfers between devices, swap(): return lax.ppermute(value, axis, [(i, i ^ mask) for i in range(n)])  3.38 us
    ppermute x3, starting transfers between devices, from_upper(): return lax.ppermute(value, both, pairs)  0.72 us
  transfers between devices with their start and end apart: 15, of which 2 were waited for; matrix products, arithmetic and copies ran while one was open for 0% of the time, Pallas kernels for 6%

profile of v1, /device:TPU:0, one launch (start us, length us, event | category | flops | bytes accessed | tf_op | source)
XLA Modules:
  0.0 26.9 jit_solution(3238658987192507359)
XLA Ops:
  0.6 1.2 %shard_map.57 = (f32[14,4,256]{2,1,0:T(4,128)S(1)}, f32[3,2,3,3,2,1,256]{6,5,4,3,2,1,0:T(1,128)S(1)}) custom-call(f32[2,3,3,2,4,256]{5,4,3,2,1,0:T(4,128)} %time_ref.3, f32[3,2,3,3,2,4,256]{6,5,4,3,2,1,0:T(4,128)} %space_ref.5), custom_call_target="tpu_custom_call" | custom-call | tf_op jit(solution)/shard_map/pallas_call | solution.py:264
  1.8 0.6 %collective-permute-start.7 = (f32[3,2,3,3,2,1,256]{6,5,4,3,2,1,0:T(1,128)S(1)}, f32[3,2,3,3,2,1,256]{6,5,4,3,2,1,0:T(1,128)S(1)}, u32[]{:S(2)}, u32[]{:S(2)}) collective-permute-start(f32[3,2,3,3,2,1,256]{6,5,4,3,2,1,0:T(1,128)S(1)} %get-tuple-element.23), channel_id=1, source_target_pairs={{1,0},{0,1},{3,2},{2,3},{5,4},{4,5},{7,6},{6,7},{9,8},{8,9},{11,10... | collective-permute-start | bytes 331784 | tf_op jit(solution)/shard_map/ppermute | solution.py:292
  2.4 2.6 %collective-permute-start = (f32[14,4,256]{2,1,0:T(4,128)S(1)}, f32[14,4,256]{2,1,0:T(4,128)S(1)}, u32[]{:S(2)}, u32[]{:S(2)}) collective-permute-start(f32[14,4,256]{2,1,0:T(4,128)S(1)} %get-tuple-element.16.refs_0_), channel_id=1, source_target_pairs={{0,2},{2,0},{4,6},{6,4},{8,10},{10,8},{12,14},{14,12},{16,18},{18,... | collective-permute-start | bytes 172040 | tf_op jit(solution)/shard_map/ppermute | solution.py:286
  5.0 1.5 %collective-permute-start.1 = (f32[14,4,256]{2,1,0:T(4,128)S(1)}, f32[14,4,256]{2,1,0:T(4,128)S(1)}, u32[]{:S(2)}, u32[]{:S(2)}) collective-permute-start(f32[14,4,256]{2,1,0:T(4,128)S(1)} %get-tuple-element.16.refs_0_), channel_id=1, source_target_pairs={{0,4},{2,6},{4,0},{6,2},{8,12},{10,14},{12,8},{14,10},{16,20},{18,... | collective-permute-start | bytes 172040 | tf_op jit(solution)/shard_map/ppermute | solution.py:286
  6.5 0.0 collective-permute-start.2
  6.5 0.0 collective-permute-done.7.time_up_ref.above_ref
  6.5 1.4 %shard_map.61 = (f32[2,4]{1,0:T(2,128)}, f32[1,128]{1,0:T(1,128)S(1)}) custom-call(f32[3,2,3,3,2,4,256]{6,5,4,3,2,1,0:T(4,128)S(1)} %copy-done, f32[3,2,3,3,2,1,256]{6,5,4,3,2,1,0:T(1,128)S(1)} %collective-permute-done.7.time_up_ref.above_ref), custom_call_target="tpu_custom_call" | custom-call | tf_op jit(solution)/shard_map/pallas_call | solution.py:264
  7.9 1.9 %collective-permute-start.9 = (f32[1,128]{1,0:T(1,128)S(1)}, f32[1,128]{1,0:T(1,128)S(1)}, u32[]{:S(2)}, u32[]{:S(2)}) collective-permute-start(f32[1,128]{1,0:T(1,128)S(1)} %get-tuple-element.27), channel_id=1, source_target_pairs={{0,2},{1,3},{2,0},{3,1},{4,6},{5,7},{6,4},{7,5},{8,10},{9,11},{10,... | collective-permute-start | bytes 1544 | tf_op jit(solution)/shard_map/ppermute | solution.py:286
  9.9 0.0 collective-permute-start.10
  9.9 0.0 collective-permute-done.refs_1_
  9.9 0.2 collective-permute-start.8
  10.1 0.0 collective-permute-done.1.refs_2_
  10.1 1.5 %collective-permute-done.2.refs_3_ = f32[14,4,256]{2,1,0:T(4,128)S(1)} collective-permute-done((f32[14,4,256]{2,1,0:T(4,128)S(1)}, f32[14,4,256]{2,1,0:T(4,128)S(1)}, u32[]{:S(2)}, u32[]{:S(2)}) %collective-permute-start.2) | collective-permute-done | bytes 57376 | tf_op jit(solution)/shard_map/ppermute | solution.py:286
  11.6 0.1 shard_map.58
  11.7 0.0 copy-start.1
  11.7 1.6 %collective-permute-start.3 = (f32[14,4,256]{2,1,0:T(4,128)S(1)}, f32[14,4,256]{2,1,0:T(4,128)S(1)}, u32[]{:S(2)}, u32[]{:S(2)}) collective-permute-start(f32[14,4,256]{2,1,0:T(4,128)S(1)} %get-tuple-element.17.mine_ref), channel_id=1, source_target_pairs={{0,8},{2,10},{4,12},{6,14},{8,0},{10,2},{12,4},{14,6},{16,24},{18,... | collective-permute-start | bytes 172040 | tf_op jit(solution)/shard_map/ppermute | solution.py:286
  13.4 0.0 collective-permute-done.9
  13.4 0.0 collective-permute-done.10
  13.4 0.0 collective-permute-done.8
  13.4 1.1 %collective-permute-start.12 = (f32[1,128]{1,0:T(1,128)S(1)}, f32[1,128]{1,0:T(1,128)S(1)}, u32[]{:S(2)}, u32[]{:S(2)}) collective-permute-start(f32[1,128]{1,0:T(1,128)S(1)} %add_add_fusion.1), channel_id=1, source_target_pairs={{0,8},{1,9},{2,10},{3,11},{4,12},{5,13},{6,14},{7,15},{8,0},{9,1},... | collective-permute-start | bytes 1544 | tf_op jit(solution)/shard_map/ppermute | solution.py:286
  14.5 1.4 %collective-permute-start.13 = (f32[1,128]{1,0:T(1,128)S(1)}, f32[1,128]{1,0:T(1,128)S(1)}, u32[]{:S(2)}, u32[]{:S(2)}) collective-permute-start(f32[1,128]{1,0:T(1,128)S(1)} %add_add_fusion.1), channel_id=1, source_target_pairs={{0,12},{1,13},{2,14},{3,15},{4,8},{5,9},{6,10},{7,11},{8,4},{9,5},... | collective-permute-start | bytes 1544 | tf_op jit(solution)/shard_map/ppermute | solution.py:286
  15.9 1.0 %collective-permute-start.11 = (f32[1,128]{1,0:T(1,128)S(1)}, f32[1,128]{1,0:T(1,128)S(1)}, u32[]{:S(2)}, u32[]{:S(2)}) collective-permute-start(f32[1,128]{1,0:T(1,128)S(1)} %add_add_fusion.1), channel_id=1, source_target_pairs={{0,4},{1,5},{2,6},{3,7},{4,0},{5,1},{6,2},{7,3},{8,12},{9,13},{10,... | collective-permute-start | bytes 1544 | tf_op jit(solution)/shard_map/ppermute | solution.py:286
  16.9 0.0 collective-permute-done.3.other_ref
  16.9 0.1 shard_map.59
  17.0 0.1 collective-permute-start.4
  17.1 2.7 %collective-permute-start.5 = (f32[14,4,256]{2,1,0:T(4,128)S(1)}, f32[14,4,256]{2,1,0:T(4,128)S(1)}, u32[]{:S(2)}, u32[]{:S(2)}) collective-permute-start(f32[14,4,256]{2,1,0:T(4,128)S(1)} %get-tuple-element.21), channel_id=1, source_target_pairs={{0,16},{2,18},{4,20},{6,22},{8,24},{10,26},{12,28},{14,30},{16,0},... | collective-permute-start | bytes 172040 | tf_op jit(solution)/shard_map/ppermute | solution.py:286
  19.8 0.0 collective-permute-done.12
  19.8 0.1 collective-permute-start.6
  19.8 0.0 collective-permute-done.13
  19.9 2.7 %collective-permute-start.14 = (f32[1,128]{1,0:T(1,128)S(1)}, f32[1,128]{1,0:T(1,128)S(1)}, u32[]{:S(2)}, u32[]{:S(2)}) collective-permute-start(f32[1,128]{1,0:T(1,128)S(1)} %add_add_fusion), channel_id=1, source_target_pairs={{0,16},{1,17},{2,18},{3,19},{4,20},{5,21},{6,22},{7,23},{8,24},{9,... | collective-permute-start | bytes 1544 | tf_op jit(solution)/shard_map/ppermute | solution.py:286
  22.5 1.9 %collective-permute-done.14 = f32[1,128]{1,0:T(1,128)S(1)} collective-permute-done((f32[1,128]{1,0:T(1,128)S(1)}, f32[1,128]{1,0:T(1,128)S(1)}, u32[]{:S(2)}, u32[]{:S(2)}) %collective-permute-start.14) | collective-permute-done | bytes 544 | tf_op jit(solution)/shard_map/ppermute | solution.py:286
  24.5 1.3 %shard_map.60 = (f32[2,3,3,2,4,256]{5,4,3,2,1,0:T(4,128)}, f32[3,2,3,3,2,4,256]{6,5,4,3,2,1,0:T(4,128)}) custom-call(s32[1]{0:T(128)} %bitcast.bit_ref, f32[2,3,3,4,256]{4,3,2,1,0:T(4,128)S(1)} %get-tuple-element.19.excl_ref, f32[2,3,3,1,256]{4,3,2,1,0:T(1,128)S(1)} %collective-permute-done.4.excl_up_ref, f32[14,4,256]{2,1,0:T(4,128)S(1)} %collective-permute-done.5.got_ref, ...), custom_call_target="tpu_custom_call" | custom-call | tf_op jit(solution)/shard_map/pallas_call | solution.py:264
  (10 shorter events, 0.0 us)
Async XLA Ops:
  0.6 5.9 %copy-start = (f32[3,2,3,3,2,4,256]{6,5,4,3,2,1,0:T(4,128)S(1)}, f32[3,2,3,3,2,4,256]{6,5,4,3,2,1,0:T(4,128)}, u32[]{:S(2)}) copy-start(f32[3,2,3,3,2,4,256]{6,5,4,3,2,1,0:T(4,128)} %space_ref.5) | copy-start | bytes 1327108
  1.8 4.7 %collective-permute-start.7 = (f32[3,2,3,3,2,1,256]{6,5,4,3,2,1,0:T(1,128)S(1)}, f32[3,2,3,3,2,1,256]{6,5,4,3,2,1,0:T(1,128)S(1)}, u32[]{:S(2)}, u32[]{:S(2)}) collective-permute-start(f32[3,2,3,3,2,1,256]{6,5,4,3,2,1,0:T(1,128)S(1)} %get-tuple-element.23), channel_id=1, source_target_pairs={{1,0},{0,1},{3,2},{2,3},{5,4},{4,5},{7,6},{6,7},{9,8},{8,9},{11,10... | collective-permute-start | bytes 331784 | tf_op jit(solution)/shard_map/ppermute | solution.py:292
  2.4 7.5 %collective-permute-start = (f32[14,4,256]{2,1,0:T(4,128)S(1)}, f32[14,4,256]{2,1,0:T(4,128)S(1)}, u32[]{:S(2)}, u32[]{:S(2)}) collective-permute-start(f32[14,4,256]{2,1,0:T(4,128)S(1)} %get-tuple-element.16.refs_0_), channel_id=1, source_target_pairs={{0,2},{2,0},{4,6},{6,4},{8,10},{10,8},{12,14},{14,12},{16,18},{18,... | collective-permute-start | bytes 172040 | tf_op jit(solution)/shard_map/ppermute | solution.py:286
  5.0 5.1 %collective-permute-start.1 = (f32[14,4,256]{2,1,0:T(4,128)S(1)}, f32[14,4,256]{2,1,0:T(4,128)S(1)}, u32[]{:S(2)}, u32[]{:S(2)}) collective-permute-start(f32[14,4,256]{2,1,0:T(4,128)S(1)} %get-tuple-element.16.refs_0_), channel_id=1, source_target_pairs={{0,4},{2,6},{4,0},{6,2},{8,12},{10,14},{12,8},{14,10},{16,20},{18,... | collective-permute-start | bytes 172040 | tf_op jit(solution)/shard_map/ppermute | solution.py:286
  6.5 5.1 %collective-permute-start.2 = (f32[14,4,256]{2,1,0:T(4,128)S(1)}, f32[14,4,256]{2,1,0:T(4,128)S(1)}, u32[]{:S(2)}, u32[]{:S(2)}) collective-permute-start(f32[14,4,256]{2,1,0:T(4,128)S(1)} %get-tuple-element.16.refs_0_), channel_id=1, source_target_pairs={{0,6},{2,4},{4,2},{6,0},{8,14},{10,12},{12,10},{14,8},{16,22},{18,... | collective-permute-start | bytes 172040 | tf_op jit(solution)/shard_map/ppermute | solution.py:286
  7.9 5.4 %collective-permute-start.9 = (f32[1,128]{1,0:T(1,128)S(1)}, f32[1,128]{1,0:T(1,128)S(1)}, u32[]{:S(2)}, u32[]{:S(2)}) collective-permute-start(f32[1,128]{1,0:T(1,128)S(1)} %get-tuple-element.27), channel_id=1, source_target_pairs={{0,2},{1,3},{2,0},{3,1},{4,6},{5,7},{6,4},{7,5},{8,10},{9,11},{10,... | collective-permute-start | bytes 1544 | tf_op jit(solution)/shard_map/ppermute | solution.py:286
  9.9 3.5 %collective-permute-start.10 = (f32[1,128]{1,0:T(1,128)S(1)}, f32[1,128]{1,0:T(1,128)S(1)}, u32[]{:S(2)}, u32[]{:S(2)}) collective-permute-start(f32[1,128]{1,0:T(1,128)S(1)} %get-tuple-element.27), channel_id=1, source_target_pairs={{0,3},{1,2},{2,1},{3,0},{4,7},{5,6},{6,5},{7,4},{8,11},{9,10},{10,... | collective-permute-start | bytes 1544 | tf_op jit(solution)/shard_map/ppermute | solution.py:286
  9.9 3.5 %collective-permute-start.8 = (f32[1,128]{1,0:T(1,128)S(1)}, f32[1,128]{1,0:T(1,128)S(1)}, u32[]{:S(2)}, u32[]{:S(2)}) collective-permute-start(f32[1,128]{1,0:T(1,128)S(1)} %get-tuple-element.27), channel_id=1, source_target_pairs={{0,1},{1,0},{2,3},{3,2},{4,5},{5,4},{6,7},{7,6},{8,9},{9,8},{10,11... | collective-permute-start | bytes 1544 | tf_op jit(solution)/shard_map/ppermute | solution.py:286
  11.7 12.8 %copy-start.1 = (f32[2,3,3,2,4,256]{5,4,3,2,1,0:T(4,128)S(1)}, f32[2,3,3,2,4,256]{5,4,3,2,1,0:T(4,128)}, u32[]{:S(2)}) copy-start(f32[2,3,3,2,4,256]{5,4,3,2,1,0:T(4,128)} %time_ref.3) | copy-start | bytes 442372
  11.7 5.2 %collective-permute-start.3 = (f32[14,4,256]{2,1,0:T(4,128)S(1)}, f32[14,4,256]{2,1,0:T(4,128)S(1)}, u32[]{:S(2)}, u32[]{:S(2)}) collective-permute-start(f32[14,4,256]{2,1,0:T(4,128)S(1)} %get-tuple-element.17.mine_ref), channel_id=1, source_target_pairs={{0,8},{2,10},{4,12},{6,14},{8,0},{10,2},{12,4},{14,6},{16,24},{18,... | collective-permute-start | bytes 172040 | tf_op jit(solution)/shard_map/ppermute | solution.py:286
  13.4 6.4 %collective-permute-start.12 = (f32[1,128]{1,0:T(1,128)S(1)}, f32[1,128]{1,0:T(1,128)S(1)}, u32[]{:S(2)}, u32[]{:S(2)}) collective-permute-start(f32[1,128]{1,0:T(1,128)S(1)} %add_add_fusion.1), channel_id=1, source_target_pairs={{0,8},{1,9},{2,10},{3,11},{4,12},{5,13},{6,14},{7,15},{8,0},{9,1},... | collective-permute-start | bytes 1544 | tf_op jit(solution)/shard_map/ppermute | solution.py:286
  14.5 5.3 %collective-permute-start.13 = (f32[1,128]{1,0:T(1,128)S(1)}, f32[1,128]{1,0:T(1,128)S(1)}, u32[]{:S(2)}, u32[]{:S(2)}) collective-permute-start(f32[1,128]{1,0:T(1,128)S(1)} %add_add_fusion.1), channel_id=1, source_target_pairs={{0,12},{1,13},{2,14},{3,15},{4,8},{5,9},{6,10},{7,11},{8,4},{9,5},... | collective-permute-start | bytes 1544 | tf_op jit(solution)/shard_map/ppermute | solution.py:286
  15.9 3.9 %collective-permute-start.11 = (f32[1,128]{1,0:T(1,128)S(1)}, f32[1,128]{1,0:T(1,128)S(1)}, u32[]{:S(2)}, u32[]{:S(2)}) collective-permute-start(f32[1,128]{1,0:T(1,128)S(1)} %add_add_fusion.1), channel_id=1, source_target_pairs={{0,4},{1,5},{2,6},{3,7},{4,0},{5,1},{6,2},{7,3},{8,12},{9,13},{10,... | collective-permute-start | bytes 1544 | tf_op jit(solution)/shard_map/ppermute | solution.py:286
  17.0 7.4 %collective-permute-start.4 = (f32[2,3,3,1,256]{4,3,2,1,0:T(1,128)S(1)}, f32[2,3,3,1,256]{4,3,2,1,0:T(1,128)S(1)}, u32[]{:S(2)}, u32[]{:S(2)}) collective-permute-start(f32[2,3,3,1,256]{4,3,2,1,0:T(1,128)S(1)} %get-tuple-element.20), channel_id=1, source_target_pairs={{1,0},{0,1},{3,2},{2,3},{5,4},{4,5},{7,6},{6,7},{9,8},{8,9},{11,10... | collective-permute-start | bytes 55304 | tf_op jit(solution)/shard_map/ppermute | solution.py:292
  17.1 7.4 %collective-permute-start.5 = (f32[14,4,256]{2,1,0:T(4,128)S(1)}, f32[14,4,256]{2,1,0:T(4,128)S(1)}, u32[]{:S(2)}, u32[]{:S(2)}) collective-permute-start(f32[14,4,256]{2,1,0:T(4,128)S(1)} %get-tuple-element.21), channel_id=1, source_target_pairs={{0,16},{2,18},{4,20},{6,22},{8,24},{10,26},{12,28},{14,30},{16,0},... | collective-permute-start | bytes 172040 | tf_op jit(solution)/shard_map/ppermute | solution.py:286
  19.8 4.7 %collective-permute-start.6 = (f32[2,3,3,1,256]{4,3,2,1,0:T(1,128)S(1)}, f32[2,3,3,1,256]{4,3,2,1,0:T(1,128)S(1)}, u32[]{:S(2)}, u32[]{:S(2)}) collective-permute-start(f32[2,3,3,1,256]{4,3,2,1,0:T(1,128)S(1)} %get-tuple-element.22), channel_id=1, source_target_pairs={{17,0},{16,1},{19,2},{18,3},{21,4},{20,5},{23,6},{22,7},{25,8},{24... | collective-permute-start | bytes 55304 | tf_op jit(solution)/shard_map/ppermute | solution.py:292
  19.9 4.5 %collective-permute-start.14 = (f32[1,128]{1,0:T(1,128)S(1)}, f32[1,128]{1,0:T(1,128)S(1)}, u32[]{:S(2)}, u32[]{:S(2)}) collective-permute-start(f32[1,128]{1,0:T(1,128)S(1)} %add_add_fusion), channel_id=1, source_target_pairs={{0,16},{1,17},{2,18},{3,19},{4,20},{5,21},{6,22},{7,23},{8,24},{9,... | collective-permute-start | bytes 1544 | tf_op jit(solution)/shard_map/ppermute | solution.py:286

commit v2 on v1

--- a/solution.py
+++ b/solution.py
@@ -126,12 +126,15 @@
     return jnp.concatenate([v[1:, :], above], axis=0)
 
 
-def first_kernel(time_ref, space_ref, out_ref, low_ref):
+def first_kernel(time_ref, out_ref):
     steps = time_ref.shape[3]
     run = load(time_ref, 0)
     for t in range(1, steps):
         run = product(run, load(time_ref, t))
     pack(out_ref, run)
+
+
+def low_kernel(time_ref, space_ref, low_ref):
     low_ref[0] = time_ref[..., 0:1, :]
     low_ref[1:3] = space_ref[0:2, ..., 0:1, :]
 
@@ -310,12 +313,14 @@
             return (parts[0] + parts[1]) + (parts[2] + parts[3])
 
         space_near = near(space_links)
-        total, lows = call(
-            first_kernel,
-            [packed, (3,) + time_links.shape[:4] + (1, sites)],
-            [time_links, space_links],
-            keep=(0, 1),
-        )
+        total = call(first_kernel, [packed], [time_links], keep=(0,))[0]
+        time_near = near(time_links)
+        lows = call(
+            low_kernel,
+            [(3,) + time_links.shape[:4] + (1, sites)],
+            [time_near, space_near],
+            keep=(0,),
+        )[0]
         slots = [total]
         for mask in (1, 2, 3):
             slots.append(swap(total, "ta", n_ta, mask))
@@ -346,7 +351,7 @@
             )
             total, excl = outs[0], outs[1]
         total_low, excl_low = outs[2], outs[3]
-        top = 1 << (bits - 1)
+        top = 3 << (bits - 2)
         got = swap(total, "ta", n_ta, top)
         got_up = from_upper(total_low, top)
         excl_up = from_upper(excl_low)
@@ -354,10 +359,10 @@
             part = summed(part, left[:2])
             left = left[2:]
         for mask in left:
-            more = swap(part, both, count, mask)
+            more = swap(part, both, count, mask | mask >> 1)
             part = part + more
         args = [bit(bits - 1)] + [near(v) for v in (excl, excl_up, got, got_up)]
-        args += [near(time_links), near(lows_up), space_near]
+        args += [time_near, near(lows_up), space_near]
         gauge, fixed = call(
             final_kernel,
             [time_links.shape, space_links.shape],

time: 27.1 us -> 30.6 us (1.13)
  local copies, waits for them, and re-layouts: 0.01 us -> 1.93 us
  starting transfers between devices: 17.5 us -> 18.9 us
  waiting for transfers between devices: 3.39 us -> 3.73 us
    unnamed x4 -> x8, local copies, waits for them, and re-layouts: 0.01 us -> 1.93 us
    ppermute x12, starting transfers between devices: 16.7 us -> 17.8 us  [swap(): return lax.ppermute(value, axis, [(i, i ^ mask) for i in range(n)])]
    ppermute x3, starting transfers between devices: 0.72 us -> 1.07 us  [from_upper(): return lax.ppermute(value, both, pairs)]
    ppermute x12, waiting for transfers between devices: 3.38 us -> 3.73 us  [swap(): return lax.ppermute(value, axis, [(i, i ^ mask) for i in range(n)])]
    pallas_call x5 -> x6, Pallas kernels: 4.12 us -> 3.92 us  [call(): pl.pallas_call(kernel, out_shape=[pltpu.VMEM(s, jnp.float32) if i in keep...]
  transfers between devices with their start and end apart: 15 -> 15, of which waited for: 2 -> 2; matrix products, arithmetic and copies ran while one was open for 0% -> 0% of each run, Pallas kernels for 6% -> 8%
where the time goes in v2:
time: 30.6 us; the launch traced here: 30.4 us
  starting transfers between devices  18.9 us (62%)
  Pallas kernels  3.92 us (13%)
  waiting for transfers between devices  3.73 us (12%)
  local copies, waits for them, and re-layouts  1.93 us (6%)
  between operations  1.91 us (6%)
    ppermute x12, starting transfers between devices, swap(): return lax.ppermute(value, axis, [(i, i ^ mask) for i in range(n)])  17.8 us
    pallas_call x6, Pallas kernels, call(): pl.pallas_call(kernel, out_shape=[pltpu.VMEM(s, jnp.float32) if i in keep...  3.92 us
    ppermute x12, waiting for transfers between devices, swap(): return lax.ppermute(value, axis, [(i, i ^ mask) for i in range(n)])  3.73 us
    unnamed x8, local copies, waits for them, and re-layouts  1.93 us
    ppermute x3, starting transfers between devices, from_upper(): return lax.ppermute(value, both, pairs)  1.07 us
  transfers between devices with their start and end apart: 15, of which 2 were waited for; matrix products, arithmetic and copies ran while one was open for 0% of the time, Pallas kernels for 8%

profile of v2, /device:TPU:0, one launch (start us, length us, event | category | flops | bytes accessed | tf_op | source)
XLA Modules:
  0.0 30.4 jit_solution(8388635296390939799)
XLA Ops:
  0.6 1.0 %copy-done = f32[3,2,3,3,2,4,256]{6,5,4,3,2,1,0:T(4,128)S(1)} copy-done((f32[3,2,3,3,2,4,256]{6,5,4,3,2,1,0:T(4,128)S(1)}, f32[3,2,3,3,2,4,256]{6,5,4,3,2,1,0:T(4,128)}, u32[]{:S(2)}) %copy-start) | copy-done | bytes 442392
  1.6 0.9 %copy-done.2 = f32[2,3,3,2,4,256]{5,4,3,2,1,0:T(4,128)S(1)} copy-done((f32[2,3,3,2,4,256]{5,4,3,2,1,0:T(4,128)S(1)}, f32[2,3,3,2,4,256]{5,4,3,2,1,0:T(4,128)}, u32[]{:S(2)}) %copy-start.2) | copy-done | bytes 147480
  2.6 0.1 shard_map.60
  2.6 0.6 %collective-permute-start.7 = (f32[3,2,3,3,2,1,256]{6,5,4,3,2,1,0:T(1,128)S(1)}, f32[3,2,3,3,2,1,256]{6,5,4,3,2,1,0:T(1,128)S(1)}, u32[]{:S(2)}, u32[]{:S(2)}) collective-permute-start(f32[3,2,3,3,2,1,256]{6,5,4,3,2,1,0:T(1,128)S(1)} %shard_map.60), channel_id=1, source_target_pairs={{1,0},{0,1},{3,2},{2,3},{5,4},{4,5},{7,6},{6,7},{9,8},{8,9},{11,10... | collective-permute-start | bytes 331784 | tf_op jit(solution)/shard_map/ppermute | solution.py:295
  3.2 0.9 %shard_map.57.refs_0_ = f32[14,4,256]{2,1,0:T(4,128)S(1)} custom-call(f32[2,3,3,2,4,256]{5,4,3,2,1,0:T(4,128)} %time_ref.5), custom_call_target="tpu_custom_call" | custom-call | tf_op jit(solution)/shard_map/pallas_call | solution.py:267
  4.1 2.6 %collective-permute-start = (f32[14,4,256]{2,1,0:T(4,128)S(1)}, f32[14,4,256]{2,1,0:T(4,128)S(1)}, u32[]{:S(2)}, u32[]{:S(2)}) collective-permute-start(f32[14,4,256]{2,1,0:T(4,128)S(1)} %shard_map.57.refs_0_), channel_id=1, source_target_pairs={{0,2},{2,0},{4,6},{6,4},{8,10},{10,8},{12,14},{14,12},{16,18},{18,... | collective-permute-start | bytes 172040 | tf_op jit(solution)/shard_map/ppermute | solution.py:289
  6.7 1.5 %collective-permute-start.1 = (f32[14,4,256]{2,1,0:T(4,128)S(1)}, f32[14,4,256]{2,1,0:T(4,128)S(1)}, u32[]{:S(2)}, u32[]{:S(2)}) collective-permute-start(f32[14,4,256]{2,1,0:T(4,128)S(1)} %shard_map.57.refs_0_), channel_id=1, source_target_pairs={{0,4},{2,6},{4,0},{6,2},{8,12},{10,14},{12,8},{14,10},{16,20},{18,... | collective-permute-start | bytes 172040 | tf_op jit(solution)/shard_map/ppermute | solution.py:289
  8.2 0.0 collective-permute-start.2
  8.2 0.0 collective-permute-done.7.time_up_ref.above_ref
  8.2 1.4 %shard_map.62 = (f32[2,4]{1,0:T(2,128)}, f32[1,128]{1,0:T(1,128)S(1)}) custom-call(f32[3,2,3,3,2,4,256]{6,5,4,3,2,1,0:T(4,128)S(1)} %copy-done.1, f32[3,2,3,3,2,1,256]{6,5,4,3,2,1,0:T(1,128)S(1)} %collective-permute-done.7.time_up_ref.above_ref), custom_call_target="tpu_custom_call" | custom-call | tf_op jit(solution)/shard_map/pallas_call | solution.py:267
  9.7 1.9 %collective-permute-start.9 = (f32[1,128]{1,0:T(1,128)S(1)}, f32[1,128]{1,0:T(1,128)S(1)}, u32[]{:S(2)}, u32[]{:S(2)}) collective-permute-start(f32[1,128]{1,0:T(1,128)S(1)} %get-tuple-element.23), channel_id=1, source_target_pairs={{0,2},{1,3},{2,0},{3,1},{4,6},{5,7},{6,4},{7,5},{8,10},{9,11},{10,... | collective-permute-start | bytes 1544 | tf_op jit(solution)/shard_map/ppermute | solution.py:289
  11.6 0.0 collective-permute-start.10
  11.6 0.0 collective-permute-done.refs_1_
  11.6 0.2 collective-permute-start.8
  11.8 0.0 collective-permute-done.1.refs_2_
  11.8 1.5 %collective-permute-done.2.refs_3_ = f32[14,4,256]{2,1,0:T(4,128)S(1)} collective-permute-done((f32[14,4,256]{2,1,0:T(4,128)S(1)}, f32[14,4,256]{2,1,0:T(4,128)S(1)}, u32[]{:S(2)}, u32[]{:S(2)}) %collective-permute-start.2) | collective-permute-done | bytes 57376 | tf_op jit(solution)/shard_map/ppermute | solution.py:289
  13.3 0.1 shard_map.58
  13.4 0.0 copy-start.3
  13.4 1.6 %collective-permute-start.3 = (f32[14,4,256]{2,1,0:T(4,128)S(1)}, f32[14,4,256]{2,1,0:T(4,128)S(1)}, u32[]{:S(2)}, u32[]{:S(2)}) collective-permute-start(f32[14,4,256]{2,1,0:T(4,128)S(1)} %get-tuple-element.14.mine_ref), channel_id=1, source_target_pairs={{0,8},{2,10},{4,12},{6,14},{8,0},{10,2},{12,4},{14,6},{16,24},{18,... | collective-permute-start | bytes 172040 | tf_op jit(solution)/shard_map/ppermute | solution.py:289
  15.1 0.0 collective-permute-done.9
  15.1 1.1 %collective-permute-start.12 = (f32[1,128]{1,0:T(1,128)S(1)}, f32[1,128]{1,0:T(1,128)S(1)}, u32[]{:S(2)}, u32[]{:S(2)}) collective-permute-start(f32[1,128]{1,0:T(1,128)S(1)} %add_add_fusion.1), channel_id=1, source_target_pairs={{0,8},{1,9},{2,10},{3,11},{4,12},{5,13},{6,14},{7,15},{8,0},{9,1},... | collective-permute-start | bytes 1544 | tf_op jit(solution)/shard_map/ppermute | solution.py:289
  16.3 1.4 %collective-permute-start.13 = (f32[1,128]{1,0:T(1,128)S(1)}, f32[1,128]{1,0:T(1,128)S(1)}, u32[]{:S(2)}, u32[]{:S(2)}) collective-permute-start(f32[1,128]{1,0:T(1,128)S(1)} %add_add_fusion.1), channel_id=1, source_target_pairs={{0,12},{1,13},{2,14},{3,15},{4,8},{5,9},{6,10},{7,11},{8,4},{9,5},... | collective-permute-start | bytes 1544 | tf_op jit(solution)/shard_map/ppermute | solution.py:289
  17.7 1.0 %collective-permute-start.11 = (f32[1,128]{1,0:T(1,128)S(1)}, f32[1,128]{1,0:T(1,128)S(1)}, u32[]{:S(2)}, u32[]{:S(2)}) collective-permute-start(f32[1,128]{1,0:T(1,128)S(1)} %add_add_fusion.1), channel_id=1, source_target_pairs={{0,4},{1,5},{2,6},{3,7},{4,0},{5,1},{6,2},{7,3},{8,12},{9,13},{10,... | collective-permute-start | bytes 1544 | tf_op jit(solution)/shard_map/ppermute | solution.py:289
  18.7 0.1 shard_map.59
  18.7 0.1 collective-permute-start.4
  18.8 3.2 %collective-permute-start.5 = (f32[14,4,256]{2,1,0:T(4,128)S(1)}, f32[14,4,256]{2,1,0:T(4,128)S(1)}, u32[]{:S(2)}, u32[]{:S(2)}) collective-permute-start(f32[14,4,256]{2,1,0:T(4,128)S(1)} %get-tuple-element.18), channel_id=1, source_target_pairs={{0,24},{2,26},{4,28},{6,30},{8,16},{10,18},{12,20},{14,22},{16,8},... | collective-permute-start | bytes 172040 | tf_op jit(solution)/shard_map/ppermute | solution.py:289
  22.0 0.4 %collective-permute-start.6 = (f32[2,3,3,1,256]{4,3,2,1,0:T(1,128)S(1)}, f32[2,3,3,1,256]{4,3,2,1,0:T(1,128)S(1)}, u32[]{:S(2)}, u32[]{:S(2)}) collective-permute-start(f32[2,3,3,1,256]{4,3,2,1,0:T(1,128)S(1)} %get-tuple-element.19), channel_id=1, source_target_pairs={{25,0},{24,1},{27,2},{26,3},{29,4},{28,5},{31,6},{30,7},{17,8},{16... | collective-permute-start | bytes 55304 | tf_op jit(solution)/shard_map/ppermute | solution.py:295
  22.5 3.2 %collective-permute-start.14 = (f32[1,128]{1,0:T(1,128)S(1)}, f32[1,128]{1,0:T(1,128)S(1)}, u32[]{:S(2)}, u32[]{:S(2)}) collective-permute-start(f32[1,128]{1,0:T(1,128)S(1)} %add_add_fusion), channel_id=1, source_target_pairs={{0,24},{1,25},{2,26},{3,27},{4,28},{5,29},{6,30},{7,31},{8,16},{9,... | collective-permute-start | bytes 1544 | tf_op jit(solution)/shard_map/ppermute | solution.py:289
  25.7 2.2 %collective-permute-done.14 = f32[1,128]{1,0:T(1,128)S(1)} collective-permute-done((f32[1,128]{1,0:T(1,128)S(1)}, f32[1,128]{1,0:T(1,128)S(1)}, u32[]{:S(2)}, u32[]{:S(2)}) %collective-permute-start.14) | collective-permute-done | bytes 544 | tf_op jit(solution)/shard_map/ppermute | solution.py:289
  28.0 0.0 collective-permute-done.6.got_up_ref
  28.0 0.0 collective-permute-done.5.got_ref
  28.0 1.3 %shard_map.61 = (f32[2,3,3,2,4,256]{5,4,3,2,1,0:T(4,128)}, f32[3,2,3,3,2,4,256]{6,5,4,3,2,1,0:T(4,128)}) custom-call(s32[1]{0:T(128)} %bitcast.bit_ref, f32[2,3,3,4,256]{4,3,2,1,0:T(4,128)S(1)} %get-tuple-element.16.excl_ref, f32[2,3,3,1,256]{4,3,2,1,0:T(1,128)S(1)} %collective-permute-done.4.excl_up_ref, f32[14,4,256]{2,1,0:T(4,128)S(1)} %collective-permute-done.5.got_ref, ...), custom_call_target="tpu_custom_call" | custom-call | tf_op jit(solution)/shard_map/pallas_call | solution.py:267
  (15 shorter events, 0.0 us)
Async XLA Ops:
  0.6 1.0 %copy-start = (f32[3,2,3,3,2,4,256]{6,5,4,3,2,1,0:T(4,128)S(1)}, f32[3,2,3,3,2,4,256]{6,5,4,3,2,1,0:T(4,128)}, u32[]{:S(2)}) copy-start(f32[3,2,3,3,2,4,256]{6,5,4,3,2,1,0:T(4,128)} %space_ref.5) | copy-start | bytes 1327108
  1.6 0.9 %copy-start.2 = (f32[2,3,3,2,4,256]{5,4,3,2,1,0:T(4,128)S(1)}, f32[2,3,3,2,4,256]{5,4,3,2,1,0:T(4,128)}, u32[]{:S(2)}) copy-start(f32[2,3,3,2,4,256]{5,4,3,2,1,0:T(4,128)} %time_ref.5) | copy-start | bytes 442372
  2.6 5.7 %copy-start.1 = (f32[3,2,3,3,2,4,256]{6,5,4,3,2,1,0:T(4,128)S(1)}, f32[3,2,3,3,2,4,256]{6,5,4,3,2,1,0:T(4,128)}, u32[]{:S(2)}) copy-start(f32[3,2,3,3,2,4,256]{6,5,4,3,2,1,0:T(4,128)} %space_ref.5) | copy-start | bytes 1327108
  2.6 5.6 %collective-permute-start.7 = (f32[3,2,3,3,2,1,256]{6,5,4,3,2,1,0:T(1,128)S(1)}, f32[3,2,3,3,2,1,256]{6,5,4,3,2,1,0:T(1,128)S(1)}, u32[]{:S(2)}, u32[]{:S(2)}) collective-permute-start(f32[3,2,3,3,2,1,256]{6,5,4,3,2,1,0:T(1,128)S(1)} %shard_map.60), channel_id=1, source_target_pairs={{1,0},{0,1},{3,2},{2,3},{5,4},{4,5},{7,6},{6,7},{9,8},{8,9},{11,10... | collective-permute-start | bytes 331784 | tf_op jit(solution)/shard_map/ppermute | solution.py:295
  4.1 7.5 %collective-permute-start = (f32[14,4,256]{2,1,0:T(4,128)S(1)}, f32[14,4,256]{2,1,0:T(4,128)S(1)}, u32[]{:S(2)}, u32[]{:S(2)}) collective-permute-start(f32[14,4,256]{2,1,0:T(4,128)S(1)} %shard_map.57.refs_0_), channel_id=1, source_target_pairs={{0,2},{2,0},{4,6},{6,4},{8,10},{10,8},{12,14},{14,12},{16,18},{18,... | collective-permute-start | bytes 172040 | tf_op jit(solution)/shard_map/ppermute | solution.py:289
  6.7 5.1 %collective-permute-start.1 = (f32[14,4,256]{2,1,0:T(4,128)S(1)}, f32[14,4,256]{2,1,0:T(4,128)S(1)}, u32[]{:S(2)}, u32[]{:S(2)}) collective-permute-start(f32[14,4,256]{2,1,0:T(4,128)S(1)} %shard_map.57.refs_0_), channel_id=1, source_target_pairs={{0,4},{2,6},{4,0},{6,2},{8,12},{10,14},{12,8},{14,10},{16,20},{18,... | collective-permute-start | bytes 172040 | tf_op jit(solution)/shard_map/ppermute | solution.py:289
  8.2 5.1 %collective-permute-start.2 = (f32[14,4,256]{2,1,0:T(4,128)S(1)}, f32[14,4,256]{2,1,0:T(4,128)S(1)}, u32[]{:S(2)}, u32[]{:S(2)}) collective-permute-start(f32[14,4,256]{2,1,0:T(4,128)S(1)} %shard_map.57.refs_0_), channel_id=1, source_target_pairs={{0,6},{2,4},{4,2},{6,0},{8,14},{10,12},{12,10},{14,8},{16,22},{18,... | collective-permute-start | bytes 172040 | tf_op jit(solution)/shard_map/ppermute | solution.py:289
  9.7 5.4 %collective-permute-start.9 = (f32[1,128]{1,0:T(1,128)S(1)}, f32[1,128]{1,0:T(1,128)S(1)}, u32[]{:S(2)}, u32[]{:S(2)}) collective-permute-start(f32[1,128]{1,0:T(1,128)S(1)} %get-tuple-element.23), channel_id=1, source_target_pairs={{0,2},{1,3},{2,0},{3,1},{4,6},{5,7},{6,4},{7,5},{8,10},{9,11},{10,... | collective-permute-start | bytes 1544 | tf_op jit(solution)/shard_map/ppermute | solution.py:289
  11.6 3.5 %collective-permute-start.10 = (f32[1,128]{1,0:T(1,128)S(1)}, f32[1,128]{1,0:T(1,128)S(1)}, u32[]{:S(2)}, u32[]{:S(2)}) collective-permute-start(f32[1,128]{1,0:T(1,128)S(1)} %get-tuple-element.23), channel_id=1, source_target_pairs={{0,3},{1,2},{2,1},{3,0},{4,7},{5,6},{6,5},{7,4},{8,11},{9,10},{10,... | collective-permute-start | bytes 1544 | tf_op jit(solution)/shard_map/ppermute | solution.py:289
  11.6 3.5 %collective-permute-start.8 = (f32[1,128]{1,0:T(1,128)S(1)}, f32[1,128]{1,0:T(1,128)S(1)}, u32[]{:S(2)}, u32[]{:S(2)}) collective-permute-start(f32[1,128]{1,0:T(1,128)S(1)} %get-tuple-element.23), channel_id=1, source_target_pairs={{0,1},{1,0},{2,3},{3,2},{4,5},{5,4},{6,7},{7,6},{8,9},{9,8},{10,11... | collective-permute-start | bytes 1544 | tf_op jit(solution)/shard_map/ppermute | solution.py:289
  13.4 14.6 %copy-start.3 = (f32[2,3,3,2,4,256]{5,4,3,2,1,0:T(4,128)S(1)}, f32[2,3,3,2,4,256]{5,4,3,2,1,0:T(4,128)}, u32[]{:S(2)}) copy-start(f32[2,3,3,2,4,256]{5,4,3,2,1,0:T(4,128)} %time_ref.5) | copy-start | bytes 442372
  13.4 5.2 %collective-permute-start.3 = (f32[14,4,256]{2,1,0:T(4,128)S(1)}, f32[14,4,256]{2,1,0:T(4,128)S(1)}, u32[]{:S(2)}, u32[]{:S(2)}) collective-permute-start(f32[14,4,256]{2,1,0:T(4,128)S(1)} %get-tuple-element.14.mine_ref), channel_id=1, source_target_pairs={{0,8},{2,10},{4,12},{6,14},{8,0},{10,2},{12,4},{14,6},{16,24},{18,... | collective-permute-start | bytes 172040 | tf_op jit(solution)/shard_map/ppermute | solution.py:289
  15.1 6.9 %collective-permute-start.12 = (f32[1,128]{1,0:T(1,128)S(1)}, f32[1,128]{1,0:T(1,128)S(1)}, u32[]{:S(2)}, u32[]{:S(2)}) collective-permute-start(f32[1,128]{1,0:T(1,128)S(1)} %add_add_fusion.1), channel_id=1, source_target_pairs={{0,8},{1,9},{2,10},{3,11},{4,12},{5,13},{6,14},{7,15},{8,0},{9,1},... | collective-permute-start | bytes 1544 | tf_op jit(solution)/shard_map/ppermute | solution.py:289
  16.3 6.2 %collective-permute-start.13 = (f32[1,128]{1,0:T(1,128)S(1)}, f32[1,128]{1,0:T(1,128)S(1)}, u32[]{:S(2)}, u32[]{:S(2)}) collective-permute-start(f32[1,128]{1,0:T(1,128)S(1)} %add_add_fusion.1), channel_id=1, source_target_pairs={{0,12},{1,13},{2,14},{3,15},{4,8},{5,9},{6,10},{7,11},{8,4},{9,5},... | collective-permute-start | bytes 1544 | tf_op jit(solution)/shard_map/ppermute | solution.py:289
  17.7 4.8 %collective-permute-start.11 = (f32[1,128]{1,0:T(1,128)S(1)}, f32[1,128]{1,0:T(1,128)S(1)}, u32[]{:S(2)}, u32[]{:S(2)}) collective-permute-start(f32[1,128]{1,0:T(1,128)S(1)} %add_add_fusion.1), channel_id=1, source_target_pairs={{0,4},{1,5},{2,6},{3,7},{4,0},{5,1},{6,2},{7,3},{8,12},{9,13},{10,... | collective-permute-start | bytes 1544 | tf_op jit(solution)/shard_map/ppermute | solution.py:289
  18.7 9.2 %collective-permute-start.4 = (f32[2,3,3,1,256]{4,3,2,1,0:T(1,128)S(1)}, f32[2,3,3,1,256]{4,3,2,1,0:T(1,128)S(1)}, u32[]{:S(2)}, u32[]{:S(2)}) collective-permute-start(f32[2,3,3,1,256]{4,3,2,1,0:T(1,128)S(1)} %get-tuple-element.17), channel_id=1, source_target_pairs={{1,0},{0,1},{3,2},{2,3},{5,4},{4,5},{7,6},{6,7},{9,8},{8,9},{11,10... | collective-permute-start | bytes 55304 | tf_op jit(solution)/shard_map/ppermute | solution.py:295
  18.8 9.2 %collective-permute-start.5 = (f32[14,4,256]{2,1,0:T(4,128)S(1)}, f32[14,4,256]{2,1,0:T(4,128)S(1)}, u32[]{:S(2)}, u32[]{:S(2)}) collective-permute-start(f32[14,4,256]{2,1,0:T(4,128)S(1)} %get-tuple-element.18), channel_id=1, source_target_pairs={{0,24},{2,26},{4,28},{6,30},{8,16},{10,18},{12,20},{14,22},{16,8},... | collective-permute-start | bytes 172040 | tf_op jit(solution)/shard_map/ppermute | solution.py:289
  22.0 6.0 %collective-permute-start.6 = (f32[2,3,3,1,256]{4,3,2,1,0:T(1,128)S(1)}, f32[2,3,3,1,256]{4,3,2,1,0:T(1,128)S(1)}, u32[]{:S(2)}, u32[]{:S(2)}) collective-permute-start(f32[2,3,3,1,256]{4,3,2,1,0:T(1,128)S(1)} %get-tuple-element.19), channel_id=1, source_target_pairs={{25,0},{24,1},{27,2},{26,3},{29,4},{28,5},{31,6},{30,7},{17,8},{16... | collective-permute-start | bytes 55304 | tf_op jit(solution)/shard_map/ppermute | solution.py:295
  22.5 5.4 %collective-permute-start.14 = (f32[1,128]{1,0:T(1,128)S(1)}, f32[1,128]{1,0:T(1,128)S(1)}, u32[]{:S(2)}, u32[]{:S(2)}) collective-permute-start(f32[1,128]{1,0:T(1,128)S(1)} %add_add_fusion), channel_id=1, source_target_pairs={{0,24},{1,25},{2,26},{3,27},{4,28},{5,29},{6,30},{7,31},{8,16},{9,... | collective-permute-start | bytes 1544 | tf_op jit(solution)/shard_map/ppermute | solution.py:289
